TPU v7x, 256 devices: a whole 4x4x8 slice. The times are simulated.
256 devices in a mesh: ctx: 128 (over x, y_hi, z, core), head: 2 (over y_lo).
Axes of the slice: x: 4, y: 4 (y_hi: 2, y_lo: 2; y = y_hi * 2 + y_lo), z: 8, core: 2. Of those that a mesh axis runs over, the one named last changes fastest.
Arguments:
- queries: bfloat16 [16384, 2048], P('ctx', 'head'), may hold values from -160 to 160
- rotated_keys: bfloat16 [16384, 512], P('ctx', 'head'), may hold values from -6 to 6
- value_matrix: bfloat16 [16384, 512], P('ctx', 'head'), may hold values from -6 to 6
- doc_lengths: int32 [8], replicated, may hold values from 1 to 12288, 16384 in all
- scored: int32 [512], P('ctx'), may hold values from 0 to 127, as said below
- residual: bfloat16 [512, 4096], P('ctx', 'head'), may hold values from -18 to 18
- norm_gain: float32 [4096], P('head'), may hold values from 0.5 to 1.5
- out_weight: bfloat16 [2048, 4096], P('head'), may hold values from -0.5 to 0.5
- lm_weight: bfloat16 [4096, 128256], P('head', 'ctx'), may hold values from -0.40625 to 0.40625
- token_ids: int32 [512], replicated, may hold values from 0 to 128255
- old_logp: float32 [512], replicated, may hold values from -24 to -9
- advantage: float32 [512], replicated, may hold values from -3 to 3
Outputs:
- attended: bfloat16 [16384, 2048], P('ctx', 'head')
- log_probs: float32 [512], replicated
- token_loss: float32 [512], replicated
Inputs may be any that keep to these rules, and one draw needn't show every extreme that they name: `scored`: each aligned block of 4 entries holds distinct increasing offsets. `doc_lengths`: the longest document has exactly three quarters of 16384 positions.
All inputs are finite; a program needn't handle non-finite values.
Results may differ from a plain program's by a relative error of at most 0.0065.
Values may be sent and summed in bfloat16 or wider, within the bound.
A program may use at most 128 MiB of HBM per device.

v0:
```python
import math
import jax
import jax.numpy as jnp
from jax import lax
from jax.sharding import Mesh
from jax.sharding import PartitionSpec as P

HEAD_SIZE = 128
CTX = ("ctx_0", "ctx_1", "ctx_2", "ctx_3")
CTX_HEAD = ("ctx_0", "ctx_1", "ctx_2", "ctx_3", "head")
masked_score = -1e30


def side_by_side(arrays, axis, dim, along):
    both = jnp.concatenate(arrays, axis=along)
    whole, at, outs = (lax.all_gather(both, axis, axis=dim, tiled=True), 0, [])
    for a in arrays:
        outs.append(lax.slice_in_dim(whole, at, at + a.shape[along], axis=along))
        at += a.shape[along]
    return tuple(outs)


def in_blocks(shard, dim, peers):
    before, after = (shard.shape[:dim], shard.shape[dim + 1 :])
    return jnp.moveaxis(shard.reshape(*before, peers, -1, *after), dim, 0)


def sum_at_owner(shard, axis, dim):
    pieces = in_blocks(shard, dim, lax.axis_size(axis))
    arrived = lax.all_to_all(pieces, axis, split_axis=0, concat_axis=0, tiled=True)
    return arrived.astype(jnp.float32).sum(axis=0)


def sent_to_all(shard, axis):
    peers = lax.axis_size(axis)
    return lax.all_to_all(
        jnp.broadcast_to(shard[None], (peers, *shard.shape)), axis, 0, 0, tiled=True
    )


def of_everyone(shard, axis):
    everything = sent_to_all(shard, axis)
    return jnp.sum(everything, axis=0)


def all_in_one(shard, axis):
    leaves = jax.tree.leaves(shard)
    order = sorted(range(len(leaves)), key=lambda k: -leaves[k].size)
    width = (1, *leaves[order[0]].shape)[-1]
    lines = [
        jnp.pad(leaves[k].reshape(-1), (0, -leaves[k].size % width)).reshape(-1, width)
        for k in order
    ]
    both, at, found = (lax.all_gather(jnp.concatenate(lines), axis), 0, {})
    for k, line in zip(order, lines):
        slab = both[:, at : at + len(line)].reshape(len(both), -1)
        found[k] = slab[:, : leaves[k].size].reshape(-1, *leaves[k].shape)
        at += len(line)
    numbers = iter(range(len(leaves)))
    return jax.tree.map(lambda _: found[next(numbers)], shard)


def merged_by_axis(shard, axes, combine):
    for axis in axes:
        pieces = all_in_one(shard, axis)
        shard = jax.tree.map(lambda part: part[0], pieces)
        for k in range(1, lax.axis_size(axis)):
            shard = combine(shard, jax.tree.map(lambda part: part[k], pieces))
    return shard


def doc_index(positions, doc_ends):
    return jnp.sum((positions[:, None] >= doc_ends[None, :]).astype(jnp.int32), axis=1)


def attend_rows(running, context, key_part, value_part, offset):
    query_heads, query_pos, query_doc, doc_ends, first_start, skipping = context
    row_top, row_total, accumulated = running
    row_count = key_part.shape[0]
    kv_heads = query_heads.shape[1]
    key_head_rows = key_part.reshape(row_count, kv_heads, HEAD_SIZE)
    value_head_rows = value_part.reshape(row_count, kv_heads, HEAD_SIZE)
    scores = jnp.einsum(
        "qkgd,rkd->kgqr", query_heads, key_head_rows, preferred_element_type=jnp.float32
    ) * HEAD_SIZE ** (-0.5)
    key_pos = offset + jnp.arange(row_count, dtype=jnp.int32)
    allowed = (
        (key_pos[None, :] <= query_pos[:, None])
        & (key_pos[None, :] >= 0)
        & (doc_index(key_pos, doc_ends)[None, :] == query_doc[:, None])
    )
    scores = jnp.where(allowed, scores, masked_score)
    new_top = jnp.maximum(row_top, jnp.max(scores, axis=-1))
    weights = jnp.where(allowed, jnp.exp(scores - new_top[..., None]), 0.0)
    rescale = jnp.exp(row_top - new_top)
    row_total = row_total * rescale + jnp.sum(weights, axis=-1)
    update = jnp.einsum(
        "kgqr,rkd->kgqd",
        weights.astype(jnp.bfloat16),
        value_head_rows,
        preferred_element_type=jnp.float32,
    )
    accumulated = accumulated * rescale[..., None] + update
    return (new_top, row_total, accumulated)


def attend_piece(running, shard_piece, context):
    key_rows, value_rows = shard_piece
    row_count = key_rows.shape[0]
    block_rows = math.gcd(row_count, 512)
    block_count = row_count // block_rows

    def one_block(block_index, carried):
        start_row = block_index * block_rows
        key_part = lax.dynamic_slice_in_dim(key_rows, start_row, block_rows, 0)
        value_part = lax.dynamic_slice_in_dim(value_rows, start_row, block_rows, 0)
        return attend_rows(carried, context, key_part, value_part, start_row)

    return lax.fori_loop(0, block_count, one_block, running)


def combine(earlier, later):
    top_one, sum_one, target_one = earlier
    top_two, sum_two, target_two = later
    new_top = jnp.maximum(top_one, top_two)
    merged_sum = sum_one * jnp.exp(top_one - new_top) + sum_two * jnp.exp(top_two - new_top)
    return (new_top, merged_sum, target_one + target_two)


def per_device(
    queries,
    rotated_keys,
    value_matrix,
    doc_lengths,
    scored,
    residual,
    norm_gain,
    out_weight,
    lm_weight,
    token_ids,
    old_logp,
    advantage,
):
    tok_rows = queries.shape[0]
    kv_heads = rotated_keys.shape[1] // HEAD_SIZE
    group_count = queries.shape[1] // rotated_keys.shape[1]
    my_index = lax.axis_index(CTX)
    doc_ends = jnp.cumsum(doc_lengths)
    doc_starts = doc_ends - doc_lengths
    query_pos = my_index * tok_rows + jnp.arange(tok_rows, dtype=jnp.int32)
    query_doc = doc_index(query_pos, doc_ends)
    first_start = jnp.max(jnp.where(doc_starts <= query_pos[0], doc_starts, 0))
    query_heads = queries.reshape(tok_rows, kv_heads, group_count, HEAD_SIZE)
    context = (query_heads, query_pos, query_doc, doc_ends, first_start, False)
    state_shape = (kv_heads, group_count, tok_rows)
    initial = (
        jnp.full(state_shape, masked_score, jnp.float32),
        jnp.zeros(state_shape, jnp.float32),
        jnp.zeros(state_shape + (HEAD_SIZE,), jnp.float32),
    )
    row_top, row_total, accumulated = attend_piece(
        initial, side_by_side((rotated_keys, value_matrix), CTX, 0, 1), context
    )
    result = accumulated / row_total[..., None]
    attended = (
        jnp.transpose(result, (2, 0, 1, 3))
        .reshape(tok_rows, kv_heads * group_count * HEAD_SIZE)
        .astype(jnp.bfloat16)
    )
    chosen = jnp.take(attended, scored, axis=0)
    partial_value = jnp.dot(chosen, out_weight, preferred_element_type=jnp.float32)
    projected = sum_at_owner(partial_value.astype(jnp.bfloat16), "head", 1)
    hidden = residual.astype(jnp.float32) + projected
    squares = of_everyone(jnp.sum(hidden * hidden, axis=1), "head")
    full_width = hidden.shape[1] * lax.axis_size("head")
    normed = (
        hidden * lax.rsqrt(squares[:, None] / full_width + 1e-05) * norm_gain[None, :]
    ).astype(jnp.bfloat16)
    partial_logits = jnp.dot(
        lax.all_gather(normed, CTX, axis=0, tiled=True),
        lm_weight,
        preferred_element_type=jnp.float32,
    )
    logits = sum_at_owner(partial_logits.astype(jnp.bfloat16), "head", 1)
    vocab_rows = logits.shape[1]
    vocab_start = (
        my_index * vocab_rows * lax.axis_size("head") + lax.axis_index("head") * vocab_rows
    )
    local_ids = token_ids - vocab_start
    matches = local_ids[:, None] == jnp.arange(vocab_rows, dtype=jnp.int32)[None, :]
    target_part = jnp.sum(jnp.where(matches, logits, 0.0), axis=1)
    local_top = jnp.max(logits, axis=1)
    sum_part = jnp.sum(jnp.exp(logits - local_top[:, None]), axis=1)
    global_top, exp_total, target = merged_by_axis(
        (local_top, sum_part, target_part), CTX_HEAD, combine
    )
    log_probs = target - global_top - jnp.log(exp_total)
    ratio = jnp.exp(jnp.clip(log_probs - old_logp, -4.0, 4.0))
    token_loss = -jnp.minimum(ratio * advantage, jnp.clip(ratio, 0.8, 1.2) * advantage)
    return (attended, log_probs, token_loss)


def solution(mesh):
    finer = Mesh(
        mesh.devices.reshape(4, 2, 8, 2, mesh.shape["head"]),
        ("ctx_0", "ctx_1", "ctx_2", "ctx_3", "head"),
    )
    placed = (
        P(CTX, "head"),
        P(CTX, "head"),
        P(CTX, "head"),
        P(),
        P(CTX),
        P(CTX, "head"),
        P("head"),
        P("head", None),
        P("head", CTX),
        P(),
        P(),
        P(),
    )
    return jax.shard_map(
        per_device,
        mesh=finer,
        in_specs=placed,
        out_specs=(P(CTX, "head"), P(), P()),
        check_vma=False,
    )
```

profile of v0, /device:TPU:1, one launch (start us, length us, event | category | flops | bytes accessed | tf_op | source)
XLA Modules:
  0.0 491.9 jit_solution(17511669347726125021)
XLA Ops:
  10.7 1.1 copy.48
  13.5 137.7 %all-gather.14.cloned.1.call-done = bf16[16384,512]{0,1:T(8,128)(2,1)} async-done(((bf16[128,512]{0,1:T(8,128)(2,1)}), bf16[16384,512]{0,1:T(8,128)(2,1)}) %all-gather.14.cloned.1.call-update) | async-done | bytes 16777232 | tf_op jit(solution)/shard_map/all_gather | solution.py:16
  151.2 11.4 %fusion.76 = (bf16[16384,256]{0,1:T(8,128)(2,1)}, bf16[16384,256]{0,1:T(8,128)(2,1)}) fusion(bf16[16384,512]{0,1:T(8,128)(2,1)} %all-gather.14.cloned.1.call-done), kind=kLoop, calls=%fused_computation.157 | loop fusion | bytes 33554432 | tf_op jit(solution)/shard_map/slice | solution.py:18
  162.7 113.7 %while.18 = (s32[]{:T(128)}, f32[2,4,128]{2,1,0:T(4,128)S(1)}, f32[2,4,128]{2,1,0:T(4,128)S(1)}, f32[2,4,128,128]{3,2,1,0:T(8,128)S(1)}, s32[8]{0:T(128)S(1)}, /...) while((s32[]{:T(128)}, f32[2,4,128]{2,1,0:T(4,128)S(1)}, ...), condition=%wide.region_6.7_spmd.clone, body=%wide.region_2.6_spmd.clone.sunk | while | flops 275925120 | bytes 9515759 | solution.py:119
  163.1 1.1 constant_dynamic-slice_fusion.3
  166.6 1.1 constant_dynamic-slice_fusion.3
  170.2 1.1 constant_dynamic-slice_fusion.3
  173.7 1.1 constant_dynamic-slice_fusion.3
  177.3 1.1 constant_dynamic-slice_fusion.3
  180.8 1.1 constant_dynamic-slice_fusion.3
  184.4 1.1 constant_dynamic-slice_fusion.3
  187.9 1.1 constant_dynamic-slice_fusion.3
  195.0 1.1 constant_dynamic-slice_fusion.3
  198.6 1.1 constant_dynamic-slice_fusion.3
  202.1 1.1 constant_dynamic-slice_fusion.3
  205.7 1.1 constant_dynamic-slice_fusion.3
  209.3 1.1 constant_dynamic-slice_fusion.3
  212.8 1.1 constant_dynamic-slice_fusion.3
  216.4 1.1 constant_dynamic-slice_fusion.3
  219.9 1.1 constant_dynamic-slice_fusion.3
  223.5 1.1 constant_dynamic-slice_fusion.3
  227.0 1.1 constant_dynamic-slice_fusion.3
  230.6 1.1 constant_dynamic-slice_fusion.3
  234.1 1.1 constant_dynamic-slice_fusion.3
  241.2 1.1 constant_dynamic-slice_fusion.3
  244.8 1.1 constant_dynamic-slice_fusion.3
  248.3 1.1 constant_dynamic-slice_fusion.3
  251.9 1.1 constant_dynamic-slice_fusion.3
  255.5 1.1 constant_dynamic-slice_fusion.3
  259.0 1.1 constant_dynamic-slice_fusion.3
  262.6 1.1 constant_dynamic-slice_fusion.3
  266.1 1.1 constant_dynamic-slice_fusion.3
  269.7 1.1 constant_dynamic-slice_fusion.3
  273.2 1.1 constant_dynamic-slice_fusion.3
  277.6 4.6 convolution_convert_fusion
  282.2 5.1 %all_to_all.16 = bf16[2,4,2048]{2,1,0:T(4,128)(2,1)S(1)} all-to-all(bf16[2,4,2048]{2,1,0:T(4,128)(2,1)S(1)} %bitcast.366), channel_id=1, replica_groups=mesh['ctx_0'=4,'ctx_1'=2,'ctx_2'=8,'ctx_3'=2,'head'=2] {'head'}, dimensions={0} | all-to-all | bytes 65536 | tf_op jit(solution)/shard_map/all_to_all | solution.py:30
  287.5 5.0 %all_to_all.17 = f32[2,1,4]{2,1,0:T(1,128)S(1)} all-to-all(f32[2,1,4]{2,1,0:T(1,128)S(1)} %broadcast_in_dim.94), channel_id=1, replica_groups=mesh['ctx_0'=4,'ctx_1'=2,'ctx_2'=8,'ctx_3'=2,'head'=2] {'head'}, dimensions={0} | all-to-all | bytes 64 | tf_op jit(solution)/shard_map/all_to_all | solution.py:36
  293.2 116.8 %all-gather.16.cloned.1.call-done = bf16[128,4,2048]{2,1,0:T(4,128)(2,1)} async-done(((bf16[1,4,2048]{2,1,0:T(4,128)(2,1)}), bf16[128,4,2048]{2,1,0:T(4,128)(2,1)}) %all-gather.16.cloned.1.call-update) | async-done | bytes 2097168 | tf_op jit(solution)/shard_map/all_gather | solution.py:180
  410.0 2.5 reshape.1099
  412.6 4.5 convolution_convert_fusion.1
  417.1 1.2 reshape.1077
  418.3 3.6 all-to-all-start.2
  421.9 13.2 %all-to-all-done.2 = bf16[2,512,501]{1,2,0:T(8,128)(2,1)S(1)} async-done(((bf16[2,512,501]{1,2,0:T(8,128)(2,1)}), bf16[2,512,501]{1,2,0:T(8,128)(2,1)S(1)}, u32[]{:S(2)}, u32[]{:S(2)}) %all-to-all-start.2) | async-done | bytes 1026080 | tf_op jit(solution)/shard_map/all_to_all | solution.py:30
  435.7 9.6 %all-gather.6 = f32[4,3,512]{2,1,0:T(4,128)S(1)} all-gather(f32[1,3,512]{2,1,0:T(4,128)S(1)} %maximum_bitcast_fusion), channel_id=2, replica_groups=mesh['ctx_0'=4,'ctx_1'=2,'ctx_2'=8,'ctx_3'=2,'head'=2] {'ctx_0'}, dimensions={0}, use_global_device_ids=true | all-gather | bytes 30720 | tf_op jit(solution)/shard_map/all_gather | solution.py:54
  445.3 4.7 all-gather.7
  450.1 18.4 %all-gather.8 = f32[8,3,512]{2,1,0:T(4,128)S(1)} all-gather(f32[1,3,512]{2,1,0:T(4,128)S(1)} %maximum_bitcast_fusion.2), channel_id=4, replica_groups=mesh['ctx_0'=4,'ctx_1'=2,'ctx_2'=8,'ctx_3'=2,'head'=2] {'ctx_2'}, dimensions={0}, use_global_device_ids=true | all-gather | bytes 55296 | tf_op jit(solution)/shard_map/all_gather | solution.py:54
  468.6 12.6 %all-gather.9 = f32[2,3,512]{2,1,0:T(4,128)S(1)} all-gather(f32[1,3,512]{2,1,0:T(4,128)S(1)} %maximum_bitcast_fusion.3), channel_id=5, replica_groups=mesh['ctx_0'=4,'ctx_1'=2,'ctx_2'=8,'ctx_3'=2,'head'=2] {'ctx_3'}, dimensions={0}, use_global_device_ids=true | all-gather | bytes 18432 | tf_op jit(solution)/shard_map/all_gather | solution.py:54
  481.2 3.2 all-gather.10
  (412 shorter events, 87.7 us)
Async XLA Ops:
  7.2 144.1 %all-gather.14.cloned.1.call-start = ((), (), s32[]{:S(2)}) async-start(), calls=%async_computation.3 | async-start | bytes 16908288 | tf_op jit(solution)/shard_map/all_gather | solution.py:16
  9.8 400.2 %all-gather.16.cloned.1.call-start = ((), (), s32[]{:S(2)}) async-start(), calls=%async_computation.4 | async-start | bytes 2113536 | tf_op jit(solution)/shard_map/all_gather | solution.py:180
  277.0 5.2 %copy-start = (bf16[128,1024]{1,0:T(8,128)(2,1)}, bf16[128,1024]{1,0:T(8,128)(2,1)S(1)}, u32[]{:S(2)}) copy-start(bf16[128,1024]{1,0:T(8,128)(2,1)S(1)} %convert_element_type.47) | copy-start | bytes 786436
  277.6 9.8 %copy-start.1 = (bf16[4,2048]{1,0:T(4,128)(2,1)S(1)}, bf16[4,2048]{1,0:T(4,128)(2,1)}, u32[]{:S(2)}) copy-start(bf16[4,2048]{1,0:T(4,128)(2,1)} %param.19) | copy-start | bytes 49156
  277.6 14.9 %copy-start.2 = (f32[2048]{0:T(1024)S(1)}, f32[2048]{0:T(1024)}, u32[]{:S(2)}) copy-start(f32[2048]{0:T(1024)} %param.20) | copy-start | bytes 24580
  417.1 4.8 copy-start.5
  418.3 16.8 %all-to-all-start.2 = ((bf16[2,512,501]{1,2,0:T(8,128)(2,1)}), bf16[2,512,501]{1,2,0:T(8,128)(2,1)S(1)}, u32[]{:S(2)}, u32[]{:S(2)}) async-start(bf16[2,512,501]{1,2,0:T(8,128)(2,1)} %bitcast.8), calls=%async_computation.2 | async-start | bytes 2064384 | tf_op jit(solution)/shard_map/all_to_all | solution.py:30
  421.9 62.6 %copy-start.3 = (f32[512]{0:T(512)S(1)}, f32[512]{0:T(512)}, u32[]{:S(2)}) copy-start(f32[512]{0:T(512)} %param.25) | copy-start | bytes 6148
  421.9 62.6 %copy-start.4 = (f32[512]{0:T(512)S(1)}, f32[512]{0:T(512)}, u32[]{:S(2)}) copy-start(f32[512]{0:T(512)} %param.24) | copy-start | bytes 6148
Sparse Core Ops, SparseCore 0:
  12.3 138.8 all-gather.13
  293.3 116.6 all-gather.15
where the time goes:
time: 493 us; the launch traced here: 492 us
  waiting for transfers between devices  268 us (54%)
  blocking collectives  58.6 us (12%)
  matrix products  56.6 us (11%)
  local copies, waits for them, and re-layouts  53.7 us (11%)
  other arithmetic  34.8 us (7%)
  between operations  14.4 us (3%)
    all_gather x1, waiting for transfers between devices, side_by_side(): whole, at, outs = (lax.all_gather(both, axis, axis=dim, tiled=True), 0, [])  138 us
    all_gather x1, waiting for transfers between devices, per_device(): lax.all_gather(normed, CTX, axis=0, tiled=True)  117 us
    all_gather x5, blocking collectives, all_in_one(): both, at, found = (lax.all_gather(jnp.concatenate(lines), axis), 0, {})  48.5 us
    dynamic_slice x32, local copies, waits for them, and re-layouts, one_block(): value_part = lax.dynamic_slice_in_dim(value_rows, start_row, block_rows, 0)  34.3 us
    dot_general x32, matrix products, attend_rows(): jnp.einsum('kgqr,rkd->kgqd', weights.astype(jnp.bfloat16), value_head_row...  30.3 us
    dot_general x32, matrix products, attend_rows(): jnp.einsum('qkgd,rkd->kgqr', query_heads, key_head_rows, preferred_elemen...  17.2 us
    reduce_sum x32, other arithmetic, attend_rows(): row_total = row_total * rescale + jnp.sum(weights, axis=-1)  16.7 us
    all_to_all x1, waiting for transfers between devices, sum_at_owner(): lax.all_to_all(pieces, axis, split_axis=0, concat_axis=0, tiled=True)  13.2 us
  transfers between devices with their start and end apart: 3, of which 3 were waited for; matrix products, arithmetic and copies ran while one was open for 1% of the time, Pallas kernels for 0%

commit v1 on v0

--- a/solution.py
+++ b/solution.py
@@ -177,7 +177,9 @@
         hidden * lax.rsqrt(squares[:, None] / full_width + 1e-05) * norm_gain[None, :]
     ).astype(jnp.bfloat16)
     partial_logits = jnp.dot(
-        lax.all_gather(normed, CTX, axis=0, tiled=True),
+        jnp.concatenate(
+            lax.all_to_all(jnp.stack([normed] * lax.axis_size(CTX)), CTX, 0, 0), axis=0
+        ),
         lm_weight,
         preferred_element_type=jnp.float32,
     )

time: 493 us -> 442 us (0.90)
  waiting for transfers between devices: 268 us -> 149 us
  blocking collectives: 58.6 us -> 125 us
    all_gather x1 -> x0, waiting for transfers between devices: 117 us -> none  [per_device(): lax.all_gather(normed, CTX, axis=0, tiled=True)]
    all_to_all x0 -> x1, blocking collectives: none -> 64.7 us  [per_device(): lax.all_to_all(jnp.stack([normed] * lax.axis_size(CTX)), CTX, 0, 0)]
  transfers between devices with their start and end apart: 3 -> 2, of which waited for: 3 -> 2; matrix products, arithmetic and copies ran while one was open for 1% -> 1% of each run, Pallas kernels for 0% -> 0%
where the time goes in v1:
time: 442 us; the launch traced here: 441 us
  waiting for transfers between devices  149 us (34%)
  blocking collectives  125 us (28%)
  matrix products  57.3 us (13%)
  local copies, waits for them, and re-layouts  54.3 us (12%)
  other arithmetic  34.2 us (8%)
  between operations  14.4 us (3%)
    all_gather x1, waiting for transfers between devices, side_by_side(): whole, at, outs = (lax.all_gather(both, axis, axis=dim, tiled=True), 0, [])  138 us
    all_to_all x1, blocking collectives, per_device(): lax.all_to_all(jnp.stack([normed] * lax.axis_size(CTX)), CTX, 0, 0)  64.7 us
    all_gather x5, blocking collectives, all_in_one(): both, at, found = (lax.all_gather(jnp.concatenate(lines), axis), 0, {})  50.5 us
    dynamic_slice x32, local copies, waits for them, and re-layouts, one_block(): value_part = lax.dynamic_slice_in_dim(value_rows, start_row, block_rows, 0)  34.3 us
    dot_general x32, matrix products, attend_rows(): jnp.einsum('kgqr,rkd->kgqd', weights.astype(jnp.bfloat16), value_head_row...  30.3 us
    dot_general x32, matrix products, attend_rows(): jnp.einsum('qkgd,rkd->kgqr', query_heads, key_head_rows, preferred_elemen...  17.2 us
    reduce_sum x32, other arithmetic, attend_rows(): row_total = row_total * rescale + jnp.sum(weights, axis=-1)  16.7 us
    all_to_all x1, waiting for transfers between devices, sum_at_owner(): lax.all_to_all(pieces, axis, split_axis=0, concat_axis=0, tiled=True)  11.5 us
  transfers between devices with their start and end apart: 2, of which 2 were waited for; matrix products, arithmetic and copies ran while one was open for 1% of the time, Pallas kernels for 0%

profile of v1, /device:TPU:1, one launch (start us, length us, event | category | flops | bytes accessed | tf_op | source)
XLA Modules:
  0.0 440.8 jit_solution(16072850196109958602)
XLA Ops:
  10.7 1.1 copy.48
  13.5 137.8 %all-gather.12.cloned.1.call-done = bf16[16384,512]{0,1:T(8,128)(2,1)} async-done(((bf16[128,512]{0,1:T(8,128)(2,1)}), bf16[16384,512]{0,1:T(8,128)(2,1)}) %all-gather.12.cloned.1.call-update) | async-done | bytes 16777232 | tf_op jit(solution)/shard_map/all_gather | solution.py:16
  151.2 11.4 %fusion.75 = (bf16[16384,256]{0,1:T(8,128)(2,1)}, bf16[16384,256]{0,1:T(8,128)(2,1)}) fusion(bf16[16384,512]{0,1:T(8,128)(2,1)} %all-gather.12.cloned.1.call-done), kind=kLoop, calls=%fused_computation.156 | loop fusion | bytes 33554432 | tf_op jit(solution)/shard_map/slice | solution.py:18
  162.7 113.7 %while.18 = (s32[]{:T(128)}, f32[2,4,128]{2,1,0:T(4,128)S(1)}, f32[2,4,128]{2,1,0:T(4,128)S(1)}, f32[2,4,128,128]{3,2,1,0:T(8,128)S(1)}, s32[8]{0:T(128)S(1)}, /...) while((s32[]{:T(128)}, f32[2,4,128]{2,1,0:T(4,128)S(1)}, ...), condition=%wide.region_6.7_spmd.clone, body=%wide.region_2.6_spmd.clone.sunk | while | flops 275925120 | bytes 9515759 | solution.py:119
  163.1 1.1 constant_dynamic-slice_fusion.3
  166.6 1.1 constant_dynamic-slice_fusion.3
  170.2 1.1 constant_dynamic-slice_fusion.3
  173.7 1.1 constant_dynamic-slice_fusion.3
  177.3 1.1 constant_dynamic-slice_fusion.3
  180.8 1.1 constant_dynamic-slice_fusion.3
  184.4 1.1 constant_dynamic-slice_fusion.3
  187.9 1.1 constant_dynamic-slice_fusion.3
  195.0 1.1 constant_dynamic-slice_fusion.3
  198.6 1.1 constant_dynamic-slice_fusion.3
  202.1 1.1 constant_dynamic-slice_fusion.3
  205.7 1.1 constant_dynamic-slice_fusion.3
  209.3 1.1 constant_dynamic-slice_fusion.3
  212.8 1.1 constant_dynamic-slice_fusion.3
  216.4 1.1 constant_dynamic-slice_fusion.3
  219.9 1.1 constant_dynamic-slice_fusion.3
  223.5 1.1 constant_dynamic-slice_fusion.3
  227.0 1.1 constant_dynamic-slice_fusion.3
  230.6 1.1 constant_dynamic-slice_fusion.3
  234.1 1.1 constant_dynamic-slice_fusion.3
  241.2 1.1 constant_dynamic-slice_fusion.3
  244.8 1.1 constant_dynamic-slice_fusion.3
  248.3 1.1 constant_dynamic-slice_fusion.3
  251.9 1.1 constant_dynamic-slice_fusion.3
  255.5 1.1 constant_dynamic-slice_fusion.3
  259.0 1.1 constant_dynamic-slice_fusion.3
  262.6 1.1 constant_dynamic-slice_fusion.3
  266.1 1.1 constant_dynamic-slice_fusion.3
  269.7 1.1 constant_dynamic-slice_fusion.3
  273.2 1.1 constant_dynamic-slice_fusion.3
  277.6 4.6 %convolution_convert_fusion = bf16[4,4096]{1,0:T(4,128)(2,1)S(1)} fusion(bf16[1024,4096]{1,0:T(8,128)(2,1)} %param.21, bf16[4,1024]{1,0:T(4,128)(2,1)S(1)} %gather_fusion, pred[4]{0:T(512)(128)(4,1)S(1)} %compare_and_fusion.1), kind=kOutput, calls=%fused_computation.27 | convolution fusion | flops 33574912 | bytes 8429572 | tf_op jit(solution)/shard_map/dot_general | solution.py:171
  282.2 5.1 %all_to_all.21 = bf16[2,4,2048]{2,1,0:T(4,128)(2,1)S(1)} all-to-all(bf16[2,4,2048]{2,1,0:T(4,128)(2,1)S(1)} %bitcast.364), channel_id=1, replica_groups=mesh['ctx_0'=4,'ctx_1'=2,'ctx_2'=8,'ctx_3'=2,'head'=2] {'head'}, dimensions={0} | all-to-all | bytes 65536 | tf_op jit(solution)/shard_map/all_to_all | solution.py:30
  287.5 5.0 %all_to_all.22 = f32[2,1,4]{2,1,0:T(1,128)S(1)} all-to-all(f32[2,1,4]{2,1,0:T(1,128)S(1)} %broadcast_in_dim.94), channel_id=1, replica_groups=mesh['ctx_0'=4,'ctx_1'=2,'ctx_2'=8,'ctx_3'=2,'head'=2] {'head'}, dimensions={0} | all-to-all | bytes 64 | tf_op jit(solution)/shard_map/all_to_all | solution.py:36
  293.6 64.7 %all_to_all.23 = bf16[128,4,2048]{2,1,0:T(4,128)(2,1)S(1)} all-to-all(bf16[128,4,2048]{2,1,0:T(4,128)(2,1)S(1)} %stack.2), channel_id=1, replica_groups=mesh['ctx_0'=4,'ctx_1'=2,'ctx_2'=8,'ctx_3'=2,'head'=2] {'ctx_0','ctx_1',..., dimensions={0} | all-to-all | bytes 4194304 | tf_op jit(solution)/shard_map/all_to_all | solution.py:181
  358.3 2.1 reshape.1082
  360.4 5.1 %convolution_convert_fusion.1 = bf16[512,1002]{0,1:T(8,128)(2,1)S(1)} fusion(bf16[512,2048]{1,0:T(8,128)(2,1)} %reshape.1082, bf16[2048,1002]{0,1:T(8,128)(2,1)} %param.22), kind=kOutput, calls=%fused_computation.29 | convolution fusion | flops 2101859328 | bytes 7227392 | tf_op jit(solution)/shard_map/dot_general | solution.py:179
  365.6 1.2 reshape.1083
  366.8 3.6 all-to-all-start.3
  370.4 11.5 %all-to-all-done.3 = bf16[2,512,501]{1,2,0:T(8,128)(2,1)S(1)} async-done(((bf16[2,512,501]{1,2,0:T(8,128)(2,1)}), bf16[2,512,501]{1,2,0:T(8,128)(2,1)S(1)}, u32[]{:S(2)}, u32[]{:S(2)}) %all-to-all-start.3) | async-done | bytes 1026080 | tf_op jit(solution)/shard_map/all_to_all | solution.py:30
  382.5 11.5 %all-gather.5 = f32[4,3,512]{2,1,0:T(4,128)S(1)} all-gather(f32[1,3,512]{2,1,0:T(4,128)S(1)} %maximum_bitcast_fusion), channel_id=2, replica_groups=mesh['ctx_0'=4,'ctx_1'=2,'ctx_2'=8,'ctx_3'=2,'head'=2] {'ctx_0'}, dimensions={0}, use_global_device_ids=true | all-gather | bytes 30720 | tf_op jit(solution)/shard_map/all_gather | solution.py:54
  394.0 4.7 %all-gather.6 = f32[2,3,512]{2,1,0:T(4,128)S(1)} all-gather(f32[1,3,512]{2,1,0:T(4,128)S(1)} %maximum_bitcast_fusion.1), channel_id=3, replica_groups=mesh['ctx_0'=4,'ctx_1'=2,'ctx_2'=8,'ctx_3'=2,'head'=2] {'ctx_1'}, dimensions={0}, use_global_device_ids=true | all-gather | bytes 18432 | tf_op jit(solution)/shard_map/all_gather | solution.py:54
  398.8 18.5 %all-gather.7 = f32[8,3,512]{2,1,0:T(4,128)S(1)} all-gather(f32[1,3,512]{2,1,0:T(4,128)S(1)} %maximum_bitcast_fusion.2), channel_id=4, replica_groups=mesh['ctx_0'=4,'ctx_1'=2,'ctx_2'=8,'ctx_3'=2,'head'=2] {'ctx_2'}, dimensions={0}, use_global_device_ids=true | all-gather | bytes 55296 | tf_op jit(solution)/shard_map/all_gather | solution.py:54
  417.4 12.7 %all-gather.8 = f32[2,3,512]{2,1,0:T(4,128)S(1)} all-gather(f32[1,3,512]{2,1,0:T(4,128)S(1)} %maximum_bitcast_fusion.3), channel_id=5, replica_groups=mesh['ctx_0'=4,'ctx_1'=2,'ctx_2'=8,'ctx_3'=2,'head'=2] {'ctx_3'}, dimensions={0}, use_global_device_ids=true | all-gather | bytes 18432 | tf_op jit(solution)/shard_map/all_gather | solution.py:54
  430.1 3.2 all-gather.9
  (411 shorter events, 88.1 us)
Async XLA Ops:
  7.2 144.1 %all-gather.12.cloned.1.call-start = ((), (), s32[]{:S(2)}) async-start(), calls=%async_computation.4 | async-start | bytes 16908288 | tf_op jit(solution)/shard_map/all_gather | solution.py:16
  277.0 5.2 %copy-start = (bf16[128,1024]{1,0:T(8,128)(2,1)}, bf16[128,1024]{1,0:T(8,128)(2,1)S(1)}, u32[]{:S(2)}) copy-start(bf16[128,1024]{1,0:T(8,128)(2,1)S(1)} %convert_element_type.47) | copy-start | bytes 786436
  277.6 9.8 %copy-start.1 = (bf16[4,2048]{1,0:T(4,128)(2,1)S(1)}, bf16[4,2048]{1,0:T(4,128)(2,1)}, u32[]{:S(2)}) copy-start(bf16[4,2048]{1,0:T(4,128)(2,1)} %param.19) | copy-start | bytes 49156
  277.6 14.9 %copy-start.2 = (f32[2048]{0:T(1024)S(1)}, f32[2048]{0:T(1024)}, u32[]{:S(2)}) copy-start(f32[2048]{0:T(1024)} %param.20) | copy-start | bytes 24580
  365.6 4.8 %copy-start.5 = (s32[512]{0:T(512)S(1)}, s32[512]{0:T(512)}, u32[]{:S(2)}) copy-start(s32[512]{0:T(512)} %param.23) | copy-start | bytes 6148
  366.8 15.1 %all-to-all-start.3 = ((bf16[2,512,501]{1,2,0:T(8,128)(2,1)}), bf16[2,512,501]{1,2,0:T(8,128)(2,1)S(1)}, u32[]{:S(2)}, u32[]{:S(2)}) async-start(bf16[2,512,501]{1,2,0:T(8,128)(2,1)} %bitcast.7), calls=%async_computation.3 | async-start | bytes 2064384 | tf_op jit(solution)/shard_map/all_to_all | solution.py:30
  370.4 62.9 %copy-start.3 = (f32[512]{0:T(512)S(1)}, f32[512]{0:T(512)}, u32[]{:S(2)}) copy-start(f32[512]{0:T(512)} %param.25) | copy-start | bytes 6148
  370.4 62.9 %copy-start.4 = (f32[512]{0:T(512)S(1)}, f32[512]{0:T(512)}, u32[]{:S(2)}) copy-start(f32[512]{0:T(512)} %param.24) | copy-start | bytes 6148
Sparse Core Ops, SparseCore 0:
  12.3 138.8 all-gather.11
